TPU v7x, 256 devices: a whole 4x4x8 slice. The times are simulated.
256 devices in a mesh: lon: 32 (over x_hi, z, core), lat: 8 (over y, x_lo).
Axes of the slice: x: 4 (x_hi: 2, x_lo: 2; x = x_hi * 2 + x_lo), y: 4, z: 8, core: 2. Of those that a mesh axis runs over, the one named last changes fastest.
Arguments:
- tokens: bfloat16 [2, 96, 147456], P(None, 'lat', 'lon'), may hold values from -6 to 6
- cotangent: bfloat16 [2, 48, 147456], P(None, 'lat', 'lon'), may hold values from -6 to 6
- kinds_one: int32 [1, 16], P(None, 'lat'), may hold values from 0 to 7
- kinds_two: int32 [1, 8], P(None, 'lat'), may hold values from 0 to 7
- table_one: float32 [8, 6, 3312], replicated, may hold values from -2 to 260
- table_two: float32 [8, 12, 3312], replicated, may hold values from -2 to 260
- gain_one: float32 [192], replicated, may hold values from 0.1 to 1.9
- gain_merge: float32 [768], replicated, may hold values from 0.1 to 1.9
- gain_two: float32 [384], replicated, may hold values from 0.1 to 1.9
- qkv_one: bfloat16 [192, 576], replicated, may hold values from -0.4375 to 0.4375
- proj_one: bfloat16 [192, 192], replicated, may hold values from -0.4375 to 0.4375
- merge_weight: bfloat16 [768, 384], replicated, may hold values from -0.21875 to 0.21875
- qkv_two: bfloat16 [384, 1152], replicated, may hold values from -0.3125 to 0.3125
- proj_two: bfloat16 [384, 384], replicated, may hold values from -0.3125 to 0.3125
Outputs:
- result: bfloat16 [2, 48, 147456], P(None, 'lat', 'lon')
- d_tokens: bfloat16 [2, 96, 147456], P(None, 'lat', 'lon')
- grad_qkv_one: bfloat16 [192, 576], replicated
- grad_proj_one: bfloat16 [192, 192], replicated
- grad_merge: bfloat16 [768, 384], replicated
- grad_qkv_two: bfloat16 [384, 1152], replicated
- grad_proj_two: bfloat16 [384, 384], replicated
All inputs are finite; a program needn't handle non-finite values.
Results may differ from a plain program's by a relative error of at most 0.025.
Values may be sent and summed in bfloat16 or wider, within the bound.
A program may use at most 128 MiB of HBM per device.

v0:
```python
import jax
import jax.numpy as jnp
import numpy as np
from jax import lax
from jax.sharding import PartitionSpec as P

C1 = 192
HEADS1 = 6
HEADS2 = 12
WIN_Z = 2
WIN_LAT = 6
WIN_LON = 12
LEVELS = 2
norm_epsilon = 1e-05
grad_epsilon = 1e-06
masked_score = -1e30


def as_sent(value):
    return jax.tree.map(lambda a: a.astype(jnp.bfloat16) if a.dtype == jnp.float32 else a, value)


def shifted_2(block, axis, distance):
    devices = range(lax.axis_size(axis))
    route = [((i - distance) % len(devices), i) for i in devices]
    return lax.ppermute(block, axis, route)


def relative_table():
    window_size = WIN_Z * WIN_LAT * WIN_LON
    positions = np.arange(window_size)
    level_at = positions // (WIN_LAT * WIN_LON)
    row_at = positions // WIN_LON % WIN_LAT
    col_at = positions % WIN_LON
    joined = (level_at[:, None] * WIN_Z + level_at[None, :]) * (WIN_LAT * WIN_LAT)
    joined = joined + row_at[:, None] * WIN_LAT + row_at[None, :]
    joined = joined * (2 * WIN_LON - 1) + col_at[:, None] - col_at[None, :] + WIN_LON - 1
    return joined.astype(np.int32)


def layer_norm(values, scaling):
    centre = jnp.mean(values, axis=-1, keepdims=True)
    spread = values - centre
    second = jnp.mean(spread * spread, axis=-1, keepdims=True)
    return spread * lax.rsqrt(second + norm_epsilon) * scaling


def to_windows(lattice):
    level_count, row_count, col_count = lattice.shape[:3]
    trailing = lattice.shape[3:]
    trailing_axes = tuple(range(6, 6 + len(trailing)))
    pieces = lattice.reshape(
        (level_count // WIN_Z, WIN_Z, row_count // WIN_LAT, WIN_LAT, col_count // WIN_LON, WIN_LON)
        + trailing
    )
    pieces = pieces.transpose((0, 2, 4, 1, 3, 5) + trailing_axes)
    return pieces.reshape(
        (
            level_count // WIN_Z,
            row_count // WIN_LAT,
            col_count // WIN_LON,
            WIN_Z * WIN_LAT * WIN_LON,
        )
        + trailing
    )


def from_windows(blocks, level_count, row_count, col_count):
    trailing = blocks.shape[4:]
    trailing_axes = tuple(range(6, 6 + len(trailing)))
    pieces = blocks.reshape(
        (level_count // WIN_Z, row_count // WIN_LAT, col_count // WIN_LON, WIN_Z, WIN_LAT, WIN_LON)
        + trailing
    )
    pieces = pieces.transpose((0, 3, 1, 4, 2, 5) + trailing_axes)
    return pieces.reshape((level_count, row_count, col_count) + trailing)


def region_codes(level_count, row_start, row_count, rows_all):
    level_index = jnp.arange(level_count, dtype=jnp.int32)
    level_part = (level_index >= level_count - WIN_Z).astype(jnp.int32) + (
        level_index >= level_count - WIN_Z // 2
    ).astype(jnp.int32)
    row_index = row_start + jnp.arange(row_count, dtype=jnp.int32)
    row_part = (row_index >= rows_all - WIN_LAT).astype(jnp.int32) + (
        row_index >= rows_all - WIN_LAT // 2
    ).astype(jnp.int32)
    return level_part[:, None] * 3 + row_part[None, :]


def attend(
    shifted,
    kind_ids,
    bias_table,
    scaling,
    w_qkv,
    w_proj,
    head_count,
    row_start,
    rows_all,
    probe_qkv,
    probe_proj,
):
    level_count, row_count, col_count, channel_count = shifted.shape
    head_size = channel_count // head_count
    base_values = shifted.astype(jnp.float32)
    normed = layer_norm(base_values, scaling).astype(jnp.bfloat16)
    flat_rows = normed.reshape(-1, channel_count)
    packed = (jnp.dot(flat_rows, w_qkv, preferred_element_type=jnp.float32) + probe_qkv).astype(
        jnp.bfloat16
    )
    packed = to_windows(packed.reshape(level_count, row_count, col_count, 3, head_count, head_size))
    query_rows = packed[..., 0, :, :]
    key_rows = packed[..., 1, :, :]
    value_rows = packed[..., 2, :, :]
    scores = jnp.einsum(
        "abdqhe,abdkhe->abdhqk", query_rows, key_rows, preferred_element_type=jnp.float32
    ) * head_size ** (-0.5)
    chosen = bias_table[kind_ids]
    full_bias = jnp.take(chosen, relative_table(), axis=3)
    scores = scores + full_bias[:, :, None]
    region_ids = region_codes(level_count, row_start, row_count, rows_all)
    tag_values = jnp.broadcast_to(
        region_ids[:, :, None], (level_count, row_count, col_count)
    ).astype(jnp.float32)
    window_tags = to_windows(tag_values)
    allowed = window_tags[..., :, None] == window_tags[..., None, :]
    scores = jnp.where(allowed[:, :, :, None], scores, masked_score)
    row_top = jnp.max(scores, axis=-1, keepdims=True)
    weights = jnp.exp(scores - row_top)
    attn_weights = (weights / jnp.sum(weights, axis=-1, keepdims=True)).astype(jnp.bfloat16)
    attended = jnp.einsum(
        "abdhqk,abdkhe->abdqhe", attn_weights, value_rows, preferred_element_type=jnp.float32
    ).astype(jnp.bfloat16)
    merged_rows = from_windows(attended, level_count, row_count, col_count).reshape(
        -1, channel_count
    )
    result = (
        base_values.reshape(-1, channel_count)
        + jnp.dot(merged_rows, w_proj, preferred_element_type=jnp.float32)
        + probe_proj
    )
    return (result.astype(jnp.bfloat16).reshape(shifted.shape), (flat_rows, merged_rows))


def merge_tokens(level_one, scaling, w_merge, probe_merge):
    level_count, row_count, col_count, channel_count = level_one.shape
    grouped = level_one.reshape(level_count, row_count // 2, 2, col_count // 2, 2, channel_count)
    grouped = grouped.transpose(0, 1, 3, 2, 4, 5).reshape(
        level_count, row_count // 2, col_count // 2, 4 * channel_count
    )
    normed = layer_norm(grouped.astype(jnp.float32), scaling).astype(jnp.bfloat16)
    flat_rows = normed.reshape(-1, 4 * channel_count)
    merged = (jnp.dot(flat_rows, w_merge, preferred_element_type=jnp.float32) + probe_merge).astype(
        jnp.bfloat16
    )
    return (
        merged.reshape(level_count, row_count // 2, col_count // 2, w_merge.shape[1]),
        flat_rows,
    )


def weight_grad(inputs, cot_rows):
    return lax.dot_general(
        inputs,
        cot_rows.astype(jnp.bfloat16),
        (((0,), (0,)), ((), ())),
        preferred_element_type=jnp.float32,
    )


def normalized(gradient):
    scale_back = lax.rsqrt(jnp.mean(gradient * gradient) + grad_epsilon)
    return (gradient * scale_back).astype(jnp.bfloat16)


def lat_move(band_piece, offset):
    return jax.tree.map(
        lambda part, own: part.astype(own.dtype),
        shifted_2(as_sent(band_piece), "lat", offset),
        band_piece,
    )


def lon_move(band_piece, offset):
    return shifted_2(as_sent(band_piece), "lon", offset).astype(band_piece.dtype)


def roll_ahead(lattice, level_step):
    half_lat = WIN_LAT // 2
    half_lon = WIN_LON // 2
    if level_step != 0:
        lattice = jnp.roll(lattice, -level_step, 0)
    lattice = jnp.concatenate([lattice[:, half_lat:], lat_move(lattice[:, :half_lat], -1)], 1)
    return jnp.concatenate([lattice[:, :, half_lon:], lon_move(lattice[:, :, :half_lon], -1)], 2)


def roll_behind(lattice, level_step):
    half_lat = WIN_LAT // 2
    half_lon = WIN_LON // 2
    lattice = jnp.concatenate([lat_move(lattice[:, -half_lat:], 1), lattice[:, :-half_lat]], 1)
    lattice = jnp.concatenate(
        [lon_move(lattice[:, :, -half_lon:], 1), lattice[:, :, :-half_lon]], 2
    )
    if level_step != 0:
        lattice = jnp.roll(lattice, level_step, 0)
    return lattice


def local_pass(shifted, kind_ids, bias_table, scaling, w_qkv, w_proj, head_count):
    level_count, row_count, col_count, channel_count = shifted.shape
    token_count = level_count * row_count * col_count
    row_start = lax.axis_index("lat") * row_count
    rows_all = lax.axis_size("lat") * row_count

    def local_forward(lattice, probe_qkv, probe_proj):
        return attend(
            lattice,
            kind_ids,
            bias_table,
            scaling,
            w_qkv,
            w_proj,
            head_count,
            row_start,
            rows_all,
            probe_qkv,
            probe_proj,
        )

    return jax.vjp(
        local_forward,
        shifted,
        jnp.zeros((token_count, 3 * channel_count), jnp.float32),
        jnp.zeros((token_count, channel_count), jnp.float32),
        has_aux=True,
    )


def merge_pass(level_one, scaling, w_merge):
    token_count = level_one.shape[0] * (level_one.shape[1] // 2) * (level_one.shape[2] // 2)

    def merge_forward(lattice, probe_merge):
        return merge_tokens(lattice, scaling, w_merge, probe_merge)

    return jax.vjp(
        merge_forward,
        level_one,
        jnp.zeros((token_count, w_merge.shape[1]), jnp.float32),
        has_aux=True,
    )


def shards(
    tokens,
    cotangent,
    kinds_one,
    kinds_two,
    table_one,
    table_two,
    gain_one,
    gain_merge,
    gain_two,
    qkv_one,
    proj_one,
    merge_weight,
    qkv_two,
    proj_two,
):
    row_count = tokens.shape[1]
    col_count = tokens.shape[2] // C1
    level_step = WIN_Z // 2
    lattice = tokens.reshape(LEVELS, row_count, col_count, C1)
    shifted_one = roll_ahead(lattice, level_step)
    block_one, pull_one, saved_one = local_pass(
        shifted_one, kinds_one, table_one, gain_one, qkv_one, proj_one, HEADS1
    )
    moved_one = roll_ahead(block_one, 0)
    shifted_two, pull_merge, merged_norm = merge_pass(moved_one, gain_merge, merge_weight)
    block_two, pull_two, saved_two = local_pass(
        shifted_two, kinds_two, table_two, gain_two, qkv_two, proj_two, HEADS2
    )
    level_two = roll_behind(block_two, level_step)
    d_block_two = roll_ahead(cotangent.reshape(level_two.shape), level_step)
    d_shift_two, d_packed_two, d_out_two = pull_two(d_block_two)
    raw_qkv_two = weight_grad(saved_two[0], d_packed_two)
    raw_proj_two = weight_grad(saved_two[1], d_out_two)
    d_moved_one, d_probe_merge = pull_merge(d_shift_two)
    raw_merge = weight_grad(merged_norm, d_probe_merge)
    d_block_one = roll_behind(d_moved_one, 0)
    d_shift_one, d_packed_one, d_out_one = pull_one(d_block_one)
    raw_qkv_one = weight_grad(saved_one[0], d_packed_one)
    raw_proj_one = weight_grad(saved_one[1], d_out_one)
    d_tokens = roll_behind(d_shift_one, level_step)
    raw_qkv_one, raw_proj_one, raw_merge, raw_qkv_two, raw_proj_two = lax.psum(
        (raw_qkv_one, raw_proj_one, raw_merge, raw_qkv_two, raw_proj_two), ("lon", "lat")
    )
    return (
        level_two.reshape(LEVELS, level_two.shape[1], -1),
        d_tokens.reshape(LEVELS, row_count, -1),
        normalized(raw_qkv_one),
        normalized(raw_proj_one),
        normalized(raw_merge),
        normalized(raw_qkv_two),
        normalized(raw_proj_two),
    )


def solution(mesh):
    in_specs = (
        P(None, "lat", "lon"),
        P(None, "lat", "lon"),
        P(None, "lat"),
        P(None, "lat"),
        P(),
        P(),
        P(),
        P(),
        P(),
        P(),
        P(),
        P(),
        P(),
        P(),
    )
    out_specs = (P(None, "lat", "lon"), P(None, "lat", "lon"), P(), P(), P(), P(), P())
    return jax.shard_map(shards, mesh=mesh, in_specs=in_specs, out_specs=out_specs, check_vma=False)
```

profile of v0, /device:TPU:8, one launch (start us, length us, event | category | flops | bytes accessed | tf_op | source)
XLA Modules:
  0.0 644.9 jit_solution(7995490828892708729)
XLA Ops:
  21.4 4.5 copy.138
  25.9 55.6 %gather_fusion.1 = f32[20736,2,6]{2,1,0:T(2,128)} fusion(f32[2,6,3312]{1,0,2:T(2,128)S(1)} %copy.138, s32[21504]{0:T(1024)S(1)} %pad_clamp_fusion), kind=kCustom, calls=%fused_computation.1 | custom fusion | bytes 2073600 | tf_op jit(solution)/shard_map/jvp(jit(_take))/gather | solution.py:120
  81.5 31.0 %copy.139 = f32[144,144,2,6]{0,1,3,2:T(8,128)} copy(f32[144,144,2,6]{3,2,1,0:T(2,128)} %bitcast.176) | data formatting | bytes 1990656 | tf_op jit(solution)/shard_map/jvp(jit(_take))/gather | solution.py:120
  113.1 38.8 %gather_fusion.2 = f32[20736,12]{1,0:T(8,128)} fusion(f32[12,3312]{0,1:T(8,128)S(1)} %bitcast.170, s32[21504]{0:T(1024)S(1)} %pad_clamp_fusion), kind=kCustom, calls=%fused_computation.2 | custom fusion | bytes 2073600 | tf_op jit(solution)/shard_map/jvp(jit(_take))/gather | solution.py:120
  151.9 12.2 %copy.152 = f32[144,144,12]{0,1,2:T(8,128)} copy(f32[144,144,12]{2,1,0:T(8,128)} %bitcast.177) | data formatting | bytes 1990656 | tf_op jit(solution)/shard_map/jvp(jit(_take))/gather | solution.py:120
  164.8 5.6 collective-permute-start.1
  177.0 3.9 reshape.727
  180.9 2.7 copy.134
  183.7 2.6 fusion.95
  190.2 2.9 fusion.5
  194.1 3.5 convert_reduce_fusion
  197.6 3.0 copy.192
  200.6 2.7 fusion.23
  203.4 3.1 copy.141
  206.4 2.5 copy.142
  208.9 2.6 reshape.733
  216.9 3.4 collective-permute-start.2
  231.2 5.0 collective-permute-start.3
  285.0 3.0 fusion.86
  301.6 2.6 convolution_bitcast_fusion
  307.8 6.7 %collective-permute-done.9 = bf16[2,12,6,192]{3,2,1,0:T(8,128)(2,1)S(1)} collective-permute-done((bf16[2,12,6,192]{3,2,1,0:T(8,128)(2,1)S(1)}, bf16[2,12,6,192]{3,2,1,0:T(8,128)(2,1)S(1)}, u32[]{:S(2)}, u32[]{:S(2)}) %collective-permute-start.9) | collective-permute-done | bytes 55328 | tf_op jit(solution)/shard_map/ppermute | solution.py:26
  318.1 2.4 reshape.747
  320.5 3.1 copy.165
  323.6 3.0 copy.166
  326.6 3.4 fusion.3
  335.4 4.9 copy.171
  340.3 2.5 copy.172
  342.8 2.9 reshape.751
  353.5 4.9 collective-permute-done.4
  358.7 7.3 %collective-permute-done.5 = bf16[2,6,6,384]{3,2,1,0:T(8,128)(2,1)S(1)} collective-permute-done((bf16[2,6,6,384]{3,2,1,0:T(8,128)(2,1)S(1)}, bf16[2,6,6,384]{3,2,1,0:T(8,128)(2,1)S(1)}, u32[]{:S(2)}, u32[]{:S(2)}) %collective-permute-start.5) | collective-permute-done | bytes 55328 | tf_op jit(solution)/shard_map/ppermute | solution.py:26
  367.2 6.9 %collective-permute-done.11 = bf16[2,12,6,192]{3,2,1,0:T(8,128)(2,1)S(1)} collective-permute-done((bf16[2,12,6,192]{3,2,1,0:T(8,128)(2,1)S(1)}, bf16[2,12,6,192]{3,2,1,0:T(8,128)(2,1)S(1)}, u32[]{:S(2)}, u32[]{:S(2)}) %collective-permute-start.11) | collective-permute-done | bytes 55328 | tf_op jit(solution)/shard_map/ppermute | solution.py:26
  375.6 245.0 %all-reduce.9.cloned.1.call-done = (f32[192,576]{1,0:T(8,128)}, f32[192,192]{1,0:T(8,128)}, f32[768,384]{1,0:T(8,128)}, f32[384,1152]{1,0:T(8,128)}, f32[384,384]{1,0:T(8,128)}) async-done(((f32[192,576]{1,0:T(8,128)}, f32[192,192]{1,0:T(8,128)}, f32[768,384]{1,0:T(8,128)}, f32[384,1152]{1,0:T(8,128)}, f32[384,384]{1,0:T(8,128)}), (f32[192,576]{1,0:T(8,128)}, f32[192,192]{1,0:T(8,128)}, ...) | async-done | bytes 4128784 | tf_op jit(solution)/shard_map/psum | solution.py:295
  (347 shorter events, 140.9 us)
Async XLA Ops:
  7.2 11.0 %copy-start = (f32[8,12,3312]{2,0,1:T(8,128)S(1)}, f32[8,12,3312]{2,0,1:T(8,128)}, u32[]{:S(2)}) copy-start(f32[8,12,3312]{2,0,1:T(8,128)} %param.21) | copy-start | bytes 3815428
  7.2 8.2 %copy-start.64 = (s32[20736]{0:T(1024)S(1)}, s32[20736]{0:T(1024)}, u32[]{:S(2)}) copy-start(s32[20736]{0:T(1024)} %constant.166) | copy-start | bytes 248836
  7.2 4.6 copy-start.55
  7.2 8.2 %copy-start.81 = (s32[1,2]{1,0:T(1,128)S(1)}, s32[1,2]{1,0:T(1,128)}, u32[]{:S(2)}) copy-start(s32[1,2]{1,0:T(1,128)} %param.18) | copy-start | bytes 28
  7.2 613.3 %all-reduce.9.cloned.1.call-start = ((), (), s32[]{:S(2)}) async-start(), calls=%async_computation | async-start | bytes 8454144 | tf_op jit(solution)/shard_map/psum | solution.py:295
  9.6 10.1 %copy-start.18 = (f32[8,6,3312]{2,0,1:T(8,128)S(1)}, f32[8,6,3312]{2,0,1:T(8,128)}, u32[]{:S(2)}) copy-start(f32[8,6,3312]{2,0,1:T(8,128)} %param.20) | copy-start | bytes 1907716
  10.4 154.3 %collective-permute-start = (bf16[2,3,24,192]{3,2,1,0:T(8,128)(2,1)}, bf16[2,3,24,192]{3,2,1,0:T(8,128)(2,1)S(1)}, u32[]{:S(2)}, u32[]{:S(2)}) collective-permute-start(bf16[2,3,24,192]{3,2,1,0:T(8,128)(2,1)} %slice.192), channel_id=1, source_target_pairs={{1,0},{2,1},{3,2},{4,3},{5,4},{6,5},{7,6},{0,7},{9,8},{10,9},{11,1... | collective-permute-start | bytes 165896 | tf_op jit(solution)/shard_map/ppermute | solution.py:26
  13.2 157.2 %collective-permute-start.6 = (bf16[2,3,12,384]{3,2,1,0:T(8,128)(2,1)}, bf16[2,3,12,384]{3,2,1,0:T(8,128)(2,1)}, u32[]{:S(2)}, u32[]{:S(2)}) collective-permute-start(bf16[2,3,12,384]{3,2,1,0:T(8,128)(2,1)} %get-tuple-element.59), channel_id=1, source_target_pairs={{1,0},{2,1},{3,2},{4,3},{5,4},{6,5},{7,6},{0,7},{9,8},{10,9},{11,1... | collective-permute-start | bytes 165896 | tf_op jit(solution)/shard_map/ppermute | solution.py:26
  81.5 31.0 %copy-start.49 = (f32[1,12,3312]{2,0,1:T(1,128)S(1)}, f32[1,12,3312]{2,0,1:T(1,128)}, u32[]{:S(2)}) copy-start(f32[1,12,3312]{2,0,1:T(1,128)} %constant_dynamic-slice_fusion) | copy-start | bytes 476932
  151.9 12.2 %copy-start.69 = (f32[768]{0:T(1024)S(1)}, f32[768]{0:T(1024)}, u32[]{:S(2)}) copy-start(f32[768]{0:T(1024)} %param.23) | copy-start | bytes 9220
  151.9 12.8 %copy-start.29 = (bf16[2,9,24,192]{3,2,1,0:T(8,128)(2,1)S(1)}, bf16[2,9,24,192]{3,2,1,0:T(8,128)(2,1)}, u32[]{:S(2)}) copy-start(bf16[2,9,24,192]{3,2,1,0:T(8,128)(2,1)} %slice.191) | copy-start | bytes 497668
  151.9 18.4 %copy-start.59 = (bf16[2,3,12,384]{3,2,1,0:T(8,128)(2,1)S(1)}, bf16[2,3,12,384]{3,2,1,0:T(8,128)(2,1)}, u32[]{:S(2)}) copy-start(bf16[2,3,12,384]{3,2,1,0:T(8,128)(2,1)} %get-tuple-element.58) | copy-start | bytes 165892
  164.8 8.6 %collective-permute-start.1 = (bf16[2,12,6,192]{3,2,1,0:T(8,128)(2,1)S(1)}, bf16[2,12,6,192]{3,2,1,0:T(8,128)(2,1)S(1)}, u32[]{:S(2)}, u32[]{:S(2)}) collective-permute-start(bf16[2,12,6,192]{3,2,1,0:T(8,128)(2,1)S(1)} %pad_maximum_fusion.9), channel_id=1, source_target_pairs={{8,0},{16,8},{24,16},{32,24},{40,32},{48,40},{56,48},{64,56},{72,6... | collective-permute-start | bytes 165896 | tf_op jit(solution)/shard_map/ppermute | solution.py:26
  171.9 3.7 copy-start.46
  171.9 3.7 copy-start.75
  171.9 48.5 %collective-permute-start.7 = (bf16[2,6,6,384]{3,2,1,0:T(8,128)(2,1)}, bf16[2,6,6,384]{3,2,1,0:T(8,128)(2,1)}, u32[]{:S(2)}, u32[]{:S(2)}) collective-permute-start(bf16[2,6,6,384]{3,2,1,0:T(8,128)(2,1)} %get-tuple-element.57), channel_id=1, source_target_pairs={{8,0},{16,8},{24,16},{32,24},{40,32},{48,40},{56,48},{64,56},{72,6... | collective-permute-start | bytes 165896 | tf_op jit(solution)/shard_map/ppermute | solution.py:26
  194.1 3.5 copy-start.52
  216.9 13.3 %collective-permute-start.2 = (bf16[2,3,24,192]{3,2,1,0:T(8,128)(2,1)}, bf16[2,3,24,192]{3,2,1,0:T(8,128)(2,1)}, u32[]{:S(2)}, u32[]{:S(2)}) collective-permute-start(bf16[2,3,24,192]{3,2,1,0:T(8,128)(2,1)} %slice.199), channel_id=1, source_target_pairs={{1,0},{2,1},{3,2},{4,3},{5,4},{6,5},{7,6},{0,7},{9,8},{10,9},{11,1... | collective-permute-start | bytes 165896 | tf_op jit(solution)/shard_map/ppermute | solution.py:26
  231.2 7.2 %collective-permute-start.3 = (bf16[2,12,6,192]{3,2,1,0:T(8,128)(2,1)S(1)}, bf16[2,12,6,192]{3,2,1,0:T(8,128)(2,1)S(1)}, u32[]{:S(2)}, u32[]{:S(2)}) collective-permute-start(bf16[2,12,6,192]{3,2,1,0:T(8,128)(2,1)S(1)} %pad_maximum_fusion.8), channel_id=1, source_target_pairs={{8,0},{16,8},{24,16},{32,24},{40,32},{48,40},{56,48},{64,56},{72,6... | collective-permute-start | bytes 165896 | tf_op jit(solution)/shard_map/ppermute | solution.py:26
  298.5 7.1 %collective-permute-start.8 = (bf16[2,3,24,192]{3,2,1,0:T(8,128)(2,1)}, bf16[2,3,24,192]{3,2,1,0:T(8,128)(2,1)}, u32[]{:S(2)}, u32[]{:S(2)}) collective-permute-start(bf16[2,3,24,192]{3,2,1,0:T(8,128)(2,1)} %copy.195), channel_id=1, source_target_pairs={{7,0},{0,1},{1,2},{2,3},{3,4},{4,5},{5,6},{6,7},{15,8},{8,9},{9,10... | collective-permute-start | bytes 165896 | tf_op jit(solution)/shard_map/ppermute | solution.py:26
  301.6 3.8 copy-start.44
  304.2 11.1 %copy-start.58 = (bf16[192,192]{1,0:T(8,128)(2,1)S(1)}, bf16[192,192]{1,0:T(8,128)(2,1)}, u32[]{:S(2)}) copy-start(bf16[192,192]{1,0:T(8,128)(2,1)} %param.26) | copy-start | bytes 221188
  305.4 9.1 %copy-start.32 = (bf16[12,32,144]{2,1,0:T(8,128)(2,1)}, bf16[12,32,144]{2,1,0:T(8,128)(2,1)S(1)}, u32[]{:S(2)}) copy-start(bf16[12,32,144]{2,1,0:T(8,128)(2,1)S(1)} %convolution_convert_fusion.12) | copy-start | bytes 331780
  306.5 7.9 %copy-start.30 = (bf16[2,12,24,192]{3,2,1,0:T(8,128)(2,1)}, bf16[2,12,24,192]{3,2,1,0:T(8,128)(2,1)S(1)}, u32[]{:S(2)}) copy-start(bf16[2,12,24,192]{3,2,1,0:T(8,128)(2,1)S(1)} %copy_dynamic-update-slice_fusion) | copy-start | bytes 663556
  306.6 7.8 %collective-permute-start.9 = (bf16[2,12,6,192]{3,2,1,0:T(8,128)(2,1)S(1)}, bf16[2,12,6,192]{3,2,1,0:T(8,128)(2,1)S(1)}, u32[]{:S(2)}, u32[]{:S(2)}) collective-permute-start(bf16[2,12,6,192]{3,2,1,0:T(8,128)(2,1)S(1)} %slice.217), channel_id=1, source_target_pairs={{248,0},{0,8},{8,16},{16,24},{24,32},{32,40},{40,48},{48,56},{56,6... | collective-permute-start | bytes 165896 | tf_op jit(solution)/shard_map/ppermute | solution.py:26
  352.9 5.6 collective-permute-start.4
  358.5 7.5 %collective-permute-start.5 = (bf16[2,6,6,384]{3,2,1,0:T(8,128)(2,1)S(1)}, bf16[2,6,6,384]{3,2,1,0:T(8,128)(2,1)S(1)}, u32[]{:S(2)}, u32[]{:S(2)}) collective-permute-start(bf16[2,6,6,384]{3,2,1,0:T(8,128)(2,1)S(1)} %fusion.69), channel_id=1, source_target_pairs={{248,0},{0,8},{8,16},{16,24},{24,32},{32,40},{40,48},{48,56},{56,6... | collective-permute-start | bytes 165896 | tf_op jit(solution)/shard_map/ppermute | solution.py:26
  358.6 7.5 %collective-permute-start.10 = (bf16[2,3,24,192]{3,2,1,0:T(8,128)(2,1)S(1)}, bf16[2,3,24,192]{3,2,1,0:T(8,128)(2,1)S(1)}, u32[]{:S(2)}, u32[]{:S(2)}) collective-permute-start(bf16[2,3,24,192]{3,2,1,0:T(8,128)(2,1)S(1)} %slice.219), channel_id=1, source_target_pairs={{7,0},{0,1},{1,2},{2,3},{3,4},{4,5},{5,6},{6,7},{15,8},{8,9},{9,10... | collective-permute-start | bytes 165896 | tf_op jit(solution)/shard_map/ppermute | solution.py:26
  366.2 7.9 %collective-permute-start.11 = (bf16[2,12,6,192]{3,2,1,0:T(8,128)(2,1)S(1)}, bf16[2,12,6,192]{3,2,1,0:T(8,128)(2,1)S(1)}, u32[]{:S(2)}, u32[]{:S(2)}) collective-permute-start(bf16[2,12,6,192]{3,2,1,0:T(8,128)(2,1)S(1)} %pad_maximum_fusion.7), channel_id=1, source_target_pairs={{248,0},{0,8},{8,16},{16,24},{24,32},{32,40},{40,48},{48,56},{56,6... | collective-permute-start | bytes 165896 | tf_op jit(solution)/shard_map/ppermute | solution.py:26
  620.5 8.3 %copy-start.17 = (f32[768,384]{1,0:T(8,128)S(1)}, f32[768,384]{1,0:T(8,128)}, u32[]{:S(2)}) copy-start(f32[768,384]{1,0:T(8,128)} %get-tuple-element.31) | copy-start | bytes 3538948
  624.8 6.5 %copy-start.14 = (f32[384,1152]{1,0:T(8,128)S(1)}, f32[384,1152]{1,0:T(8,128)}, u32[]{:S(2)}) copy-start(f32[384,1152]{1,0:T(8,128)} %get-tuple-element.32) | copy-start | bytes 5308420
  633.0 4.8 copy-start.1
  (63 other events, 103.1 us)
Sparse Core Ops, SparseCore 0:
  351.6 268.9 all-reduce.8
where the time goes:
time: 656 us; the launch traced here: 645 us
  waiting for transfers between devices  272 us (41%)
  local copies, waits for them, and re-layouts  246 us (38%)
  other arithmetic  46.4 us (7%)
  matrix products  40.4 us (6%)
  starting transfers between devices  20.1 us (3%)
  between operations  19.7 us (3%)
    psum x1, waiting for transfers between devices, shards(): lax.psum((raw_qkv_one, raw_proj_one, raw_merge, raw_qkv_two, raw_proj_two...  245 us
    gather x4, local copies, waits for them, and re-layouts, attend(): full_bias = jnp.take(chosen, relative_table(), axis=3)  138 us
    ppermute x12, waiting for transfers between devices, shifted_2(): return lax.ppermute(block, axis, route)  27 us
    ppermute x12, starting transfers between devices, shifted_2(): return lax.ppermute(block, axis, route)  20.1 us
    unnamed x171, local copies, waits for them, and re-layouts  18.2 us
  transfers between devices with their start and end apart: 13, of which 6 were waited for; matrix products, arithmetic and copies ran while one was open for 33% of the time, Pallas kernels for 0%

commit v1 on v0

--- a/solution.py
+++ b/solution.py
@@ -267,6 +267,12 @@
     qkv_two,
     proj_two,
 ):
+
+    def switch_regions_here(state):
+        for j0 in ("lon", "lat"):
+            state = jax.lax.psum(state, j0)
+        return state
+
     row_count = tokens.shape[1]
     col_count = tokens.shape[2] // C1
     level_step = WIN_Z // 2
@@ -292,8 +298,8 @@
     raw_qkv_one = weight_grad(saved_one[0], d_packed_one)
     raw_proj_one = weight_grad(saved_one[1], d_out_one)
     d_tokens = roll_behind(d_shift_one, level_step)
-    raw_qkv_one, raw_proj_one, raw_merge, raw_qkv_two, raw_proj_two = lax.psum(
-        (raw_qkv_one, raw_proj_one, raw_merge, raw_qkv_two, raw_proj_two), ("lon", "lat")
+    raw_qkv_one, raw_proj_one, raw_merge, raw_qkv_two, raw_proj_two = switch_regions_here(
+        (raw_qkv_one, raw_proj_one, raw_merge, raw_qkv_two, raw_proj_two)
     )
     return (
         level_two.reshape(LEVELS, level_two.shape[1], -1),

time: 656 us -> 851 us (1.30)
  waiting for transfers between devices: 272 us -> 465 us
    psum x1 -> x2, waiting for transfers between devices: 245 us -> 439 us  [switch_regions_here(): state = jax.lax.psum(state, j0)]
  transfers between devices with their start and end apart: 13 -> 14, of which waited for: 6 -> 7; matrix products, arithmetic and copies ran while one was open for 33% -> 26% of each run, Pallas kernels for 0% -> 0%
where the time goes in v1:
time: 851 us; the launch traced here: 839 us
  waiting for transfers between devices  465 us (55%)
  local copies, waits for them, and re-layouts  246 us (29%)
  other arithmetic  46.4 us (5%)
  matrix products  40.4 us (5%)
  starting transfers between devices  21.7 us (3%)
  between operations  19.7 us (2%)
    psum x2, waiting for transfers between devices, switch_regions_here(): state = jax.lax.psum(state, j0)  439 us
    gather x4, local copies, waits for them, and re-layouts, attend(): full_bias = jnp.take(chosen, relative_table(), axis=3)  138 us
    ppermute x12, waiting for transfers between devices, shifted_2(): return lax.ppermute(block, axis, route)  25.5 us
    ppermute x12, starting transfers between devices, shifted_2(): return lax.ppermute(block, axis, route)  21.6 us
    unnamed x171, local copies, waits for them, and re-layouts  18.2 us
  transfers between devices with their start and end apart: 14, of which 7 were waited for; matrix products, arithmetic and copies ran while one was open for 26% of the time, Pallas kernels for 0%

profile of v1, /device:TPU:8, one launch (start us, length us, event | category | flops | bytes accessed | tf_op | source)
XLA Modules:
  0.0 839.1 jit_solution(15603349317365039086)
XLA Ops:
  21.4 4.5 copy.138
  25.9 55.7 %gather_fusion.1 = f32[20736,2,6]{2,1,0:T(2,128)} fusion(f32[2,6,3312]{1,0,2:T(2,128)S(1)} %copy.138, s32[21504]{0:T(1024)S(1)} %pad_clamp_fusion), kind=kCustom, calls=%fused_computation.1 | custom fusion | bytes 2073600 | tf_op jit(solution)/shard_map/jvp(jit(_take))/gather | solution.py:120
  81.6 31.1 %copy.139 = f32[144,144,2,6]{0,1,3,2:T(8,128)} copy(f32[144,144,2,6]{3,2,1,0:T(2,128)} %bitcast.176) | data formatting | bytes 1990656 | tf_op jit(solution)/shard_map/jvp(jit(_take))/gather | solution.py:120
  113.2 38.8 %gather_fusion.2 = f32[20736,12]{1,0:T(8,128)} fusion(f32[12,3312]{0,1:T(8,128)S(1)} %bitcast.170, s32[21504]{0:T(1024)S(1)} %pad_clamp_fusion), kind=kCustom, calls=%fused_computation.2 | custom fusion | bytes 2073600 | tf_op jit(solution)/shard_map/jvp(jit(_take))/gather | solution.py:120
  152.0 12.2 %copy.152 = f32[144,144,12]{0,1,2:T(8,128)} copy(f32[144,144,12]{2,1,0:T(8,128)} %bitcast.177) | data formatting | bytes 1990656 | tf_op jit(solution)/shard_map/jvp(jit(_take))/gather | solution.py:120
  164.9 5.6 collective-permute-start.1
  177.1 3.9 reshape.727
  181.1 2.7 copy.134
  183.8 2.6 fusion.95
  190.3 2.9 fusion.5
  194.2 3.5 convert_reduce_fusion
  197.8 3.0 copy.192
  200.8 2.7 fusion.23
  203.5 3.1 copy.141
  206.6 2.5 copy.142
  209.0 2.6 reshape.733
  217.1 3.4 collective-permute-start.2
  231.3 5.0 collective-permute-start.3
  285.1 3.0 fusion.86
  301.7 2.6 convolution_bitcast_fusion
  307.8 6.7 collective-permute-done.9
  320.6 3.1 copy.165
  323.7 3.0 copy.166
  326.7 3.4 fusion.3
  335.5 4.9 copy.171
  340.4 2.5 copy.172
  343.0 2.9 reshape.751
  351.6 274.9 %all-reduce.11.cloned.1.call-done = (f32[192,576]{1,0:T(8,128)}, f32[192,192]{1,0:T(8,128)}, f32[768,384]{1,0:T(8,128)}, f32[384,1152]{1,0:T(8,128)}, f32[384,384]{1,0:T(8,128)}) async-done(((f32[192,576]{1,0:T(8,128)}, f32[192,192]{1,0:T(8,128)}, f32[768,384]{1,0:T(8,128)}, f32[384,1152]{1,0:T(8,128)}, f32[384,384]{1,0:T(8,128)}), (f32[192,576]{1,0:T(8,128)}, f32[192,192]{1,0:T(8,128)}, ...) | async-done | bytes 4128784 | tf_op jit(solution)/shard_map/psum | solution.py:273
  629.4 4.3 collective-permute-done.4
  634.6 6.6 collective-permute-done.5
  642.4 6.8 collective-permute-done.11
  650.7 164.0 %all-reduce.13.cloned.1.call-done = (f32[192,576]{1,0:T(8,128)}, f32[192,192]{1,0:T(8,128)}, f32[768,384]{1,0:T(8,128)}, f32[384,1152]{1,0:T(8,128)}, f32[384,384]{1,0:T(8,128)}) async-done(((f32[192,576]{1,0:T(8,128)}, f32[192,192]{1,0:T(8,128)}, f32[768,384]{1,0:T(8,128)}, f32[384,1152]{1,0:T(8,128)}, f32[384,384]{1,0:T(8,128)}), (f32[192,576]{1,0:T(8,128)}, f32[192,192]{1,0:T(8,128)}, ...) | async-done | bytes 4128784 | tf_op jit(solution)/shard_map/psum | solution.py:273
  (350 shorter events, 144.9 us)
Async XLA Ops:
  7.2 11.0 %copy-start = (f32[8,12,3312]{2,0,1:T(8,128)S(1)}, f32[8,12,3312]{2,0,1:T(8,128)}, u32[]{:S(2)}) copy-start(f32[8,12,3312]{2,0,1:T(8,128)} %param.21) | copy-start | bytes 3815428
  7.2 8.2 copy-start.64
  7.2 4.6 copy-start.55
  7.2 8.2 copy-start.81
  7.2 619.3 %all-reduce.11.cloned.1.call-start = ((), (), s32[]{:S(2)}) async-start(), calls=%async_computation | async-start | bytes 8454144 | tf_op jit(solution)/shard_map/psum | solution.py:273
  9.6 10.1 %copy-start.18 = (f32[8,6,3312]{2,0,1:T(8,128)S(1)}, f32[8,6,3312]{2,0,1:T(8,128)}, u32[]{:S(2)}) copy-start(f32[8,6,3312]{2,0,1:T(8,128)} %param.20) | copy-start | bytes 1907716
  10.4 154.4 %collective-permute-start = (bf16[2,3,24,192]{3,2,1,0:T(8,128)(2,1)}, bf16[2,3,24,192]{3,2,1,0:T(8,128)(2,1)S(1)}, u32[]{:S(2)}, u32[]{:S(2)}) collective-permute-start(bf16[2,3,24,192]{3,2,1,0:T(8,128)(2,1)} %slice.192), channel_id=1, source_target_pairs={{1,0},{2,1},{3,2},{4,3},{5,4},{6,5},{7,6},{0,7},{9,8},{10,9},{11,1... | collective-permute-start | bytes 165896 | tf_op jit(solution)/shard_map/ppermute | solution.py:26
  13.2 157.3 %collective-permute-start.6 = (bf16[2,3,12,384]{3,2,1,0:T(8,128)(2,1)}, bf16[2,3,12,384]{3,2,1,0:T(8,128)(2,1)}, u32[]{:S(2)}, u32[]{:S(2)}) collective-permute-start(bf16[2,3,12,384]{3,2,1,0:T(8,128)(2,1)} %get-tuple-element.64), channel_id=1, source_target_pairs={{1,0},{2,1},{3,2},{4,3},{5,4},{6,5},{7,6},{0,7},{9,8},{10,9},{11,1... | collective-permute-start | bytes 165896 | tf_op jit(solution)/shard_map/ppermute | solution.py:26
  81.6 31.1 %copy-start.49 = (f32[1,12,3312]{2,0,1:T(1,128)S(1)}, f32[1,12,3312]{2,0,1:T(1,128)}, u32[]{:S(2)}) copy-start(f32[1,12,3312]{2,0,1:T(1,128)} %constant_dynamic-slice_fusion) | copy-start | bytes 476932
  152.0 12.2 %copy-start.69 = (f32[768]{0:T(1024)S(1)}, f32[768]{0:T(1024)}, u32[]{:S(2)}) copy-start(f32[768]{0:T(1024)} %param.23) | copy-start | bytes 9220
  152.0 12.8 %copy-start.29 = (bf16[2,9,24,192]{3,2,1,0:T(8,128)(2,1)S(1)}, bf16[2,9,24,192]{3,2,1,0:T(8,128)(2,1)}, u32[]{:S(2)}) copy-start(bf16[2,9,24,192]{3,2,1,0:T(8,128)(2,1)} %slice.191) | copy-start | bytes 497668
  152.0 18.4 %copy-start.59 = (bf16[2,3,12,384]{3,2,1,0:T(8,128)(2,1)S(1)}, bf16[2,3,12,384]{3,2,1,0:T(8,128)(2,1)}, u32[]{:S(2)}) copy-start(bf16[2,3,12,384]{3,2,1,0:T(8,128)(2,1)} %get-tuple-element.63) | copy-start | bytes 165892
  164.9 8.6 %collective-permute-start.1 = (bf16[2,12,6,192]{3,2,1,0:T(8,128)(2,1)S(1)}, bf16[2,12,6,192]{3,2,1,0:T(8,128)(2,1)S(1)}, u32[]{:S(2)}, u32[]{:S(2)}) collective-permute-start(bf16[2,12,6,192]{3,2,1,0:T(8,128)(2,1)S(1)} %pad_maximum_fusion.9), channel_id=1, source_target_pairs={{8,0},{16,8},{24,16},{32,24},{40,32},{48,40},{56,48},{64,56},{72,6... | collective-permute-start | bytes 165896 | tf_op jit(solution)/shard_map/ppermute | solution.py:26
  172.0 3.7 copy-start.46
  172.0 3.7 copy-start.75
  172.0 48.5 %collective-permute-start.7 = (bf16[2,6,6,384]{3,2,1,0:T(8,128)(2,1)}, bf16[2,6,6,384]{3,2,1,0:T(8,128)(2,1)}, u32[]{:S(2)}, u32[]{:S(2)}) collective-permute-start(bf16[2,6,6,384]{3,2,1,0:T(8,128)(2,1)} %get-tuple-element.62), channel_id=1, source_target_pairs={{8,0},{16,8},{24,16},{32,24},{40,32},{48,40},{56,48},{64,56},{72,6... | collective-permute-start | bytes 165896 | tf_op jit(solution)/shard_map/ppermute | solution.py:26
  217.1 13.3 %collective-permute-start.2 = (bf16[2,3,24,192]{3,2,1,0:T(8,128)(2,1)}, bf16[2,3,24,192]{3,2,1,0:T(8,128)(2,1)}, u32[]{:S(2)}, u32[]{:S(2)}) collective-permute-start(bf16[2,3,24,192]{3,2,1,0:T(8,128)(2,1)} %slice.199), channel_id=1, source_target_pairs={{1,0},{2,1},{3,2},{4,3},{5,4},{6,5},{7,6},{0,7},{9,8},{10,9},{11,1... | collective-permute-start | bytes 165896 | tf_op jit(solution)/shard_map/ppermute | solution.py:26
  231.3 7.2 collective-permute-start.3
  298.6 7.1 collective-permute-start.8
  301.7 3.8 copy-start.44
  304.3 11.1 %copy-start.58 = (bf16[192,192]{1,0:T(8,128)(2,1)S(1)}, bf16[192,192]{1,0:T(8,128)(2,1)}, u32[]{:S(2)}) copy-start(bf16[192,192]{1,0:T(8,128)(2,1)} %param.26) | copy-start | bytes 221188
  305.5 9.1 %copy-start.32 = (bf16[12,32,144]{2,1,0:T(8,128)(2,1)}, bf16[12,32,144]{2,1,0:T(8,128)(2,1)S(1)}, u32[]{:S(2)}) copy-start(bf16[12,32,144]{2,1,0:T(8,128)(2,1)S(1)} %convolution_convert_fusion.12) | copy-start | bytes 331780
  306.6 7.9 copy-start.30
  306.7 7.8 collective-permute-start.9
  351.5 463.2 %all-reduce.13.cloned.1.call-start = ((), (), s32[]{:S(2)}) async-start(), calls=%async_computation.1 | async-start | bytes 8454144 | tf_op jit(solution)/shard_map/psum | solution.py:273
  628.0 5.7 collective-permute-start.4
  633.7 7.5 collective-permute-start.5
  633.8 7.5 collective-permute-start.10
  641.4 7.8 collective-permute-start.11
  814.7 8.3 copy-start.17
  819.0 6.5 copy-start.14
  827.2 4.8 copy-start.1
  (64 other events, 106.5 us)
Sparse Core Ops, SparseCore 0:
  351.7 274.8 all-reduce.10
  629.6 185.0 all-reduce.12
